TPU v7x, 32 devices: a whole 2x2x4 slice. The times are simulated.
32 devices in a mesh: dp: 8 (over y, x, core), tensor: 4 (over z).
Axes of the slice: x: 2, y: 2, z: 4, core: 2. Of those that a mesh axis runs over, the one named last changes fastest.
Arguments:
- tokens: bfloat16 [2048, 8, 1024], P('tensor', 'dp'), may hold values from -6 to 6
- weights: bfloat16 [1024, 12288], P(None, 'tensor'), may hold values from -0.71 to 0.71
- norms: float32 [4, 1024], replicated, may hold values from -0.75 to 1.5
- cotangent: bfloat16 [2048, 8, 1024], P('tensor', 'dp'), may hold values from -6 to 6
- lengths: int32 [8], P('dp'), may hold values from 512 to 2048, as said below
- owners: int32 [7], replicated, may hold values from 0 to 7, as said below
- master: float32 [8, 1024, 4096], P('dp', None, 'tensor'), may hold values from -0.05 to 0.05
- moment_one: float32 [8, 1024, 4096], P('dp', None, 'tensor'), may hold values from -24 to 24
- moment_two: float32 [8, 1024, 4096], P('dp', None, 'tensor'), may hold values from 0.5 to 8
- norm_master: float32 [8, 4, 1024], P('dp'), may hold values from 0.5 to 1.5
- norm_one: float32 [8, 4, 1024], P('dp'), may hold values from -24 to 24
- norm_two: float32 [8, 4, 1024], P('dp'), may hold values from 0.5 to 8
Outputs:
- outputs: bfloat16 [2048, 8, 1024], P('tensor', 'dp')
- input_grad: bfloat16 [2048, 8, 1024], P('tensor', 'dp')
- weight_grads: float32 [8, 1024, 4096], P('dp', None, 'tensor')
- new_master: float32 [8, 1024, 4096], P('dp', None, 'tensor')
- new_one: float32 [8, 1024, 4096], P('dp', None, 'tensor')
- new_two: float32 [8, 1024, 4096], P('dp', None, 'tensor')
- new_weights: bfloat16 [1024, 12288], P(None, 'tensor')
- norm_grads: float32 [4, 1024], replicated
- new_norm_master: float32 [8, 4, 1024], P('dp')
- new_norm_one: float32 [8, 4, 1024], P('dp')
- new_norm_two: float32 [8, 4, 1024], P('dp')
Inputs may be any that keep to these rules, and one draw needn't show every extreme that they name: `lengths`: some sequence fills all 2048 positions. The up and down matrices have different owners that own no other matrix; the four attention matrices have at most two owners between them, neither of them an owner of up or down, so no index owns more than 4 tiles of a block and the owner of up owns exactly 4.
All inputs are finite; a program needn't handle non-finite values.
Results may differ from a plain program's by a relative error of at most 0.02.
Values may be sent and summed in bfloat16 or wider, within the bound.
A program may use at most 192 MiB of HBM per device.

v0:
```python
from functools import partial
import jax
import jax.numpy as jnp
from jax import lax
from jax.sharding import PartitionSpec as P

D = 1024
FF = 4096
ADAM_STEP = 10
HEAD_DIM = 64
precise = lax.Precision.HIGHEST
beta_one = 0.9
beta_two = 0.999
learn_rate = 0.02
weight_decay = 0.1
adam_eps = 1e-08
norm_eps = 1e-05
masked_score = -1e30


def layer_norm_parts(value, gain, shift):
    average = jnp.mean(value, axis=-1, keepdims=True)
    centred = value - average
    variance = jnp.mean(centred * centred, axis=-1, keepdims=True)
    inverse = lax.rsqrt(variance + norm_eps)
    normed = centred * inverse
    return (normed * gain + shift, normed, inverse)


def layer_norm_back(upstream, normed, inverse, gain):
    scaled = upstream * gain
    inner = (
        scaled
        - jnp.mean(scaled, axis=-1, keepdims=True)
        - normed * jnp.mean(scaled * normed, axis=-1, keepdims=True)
    )
    return (inner * inverse, jnp.sum(upstream * normed, axis=0), jnp.sum(upstream, axis=0))


def slot_table(owners):
    repeat = FF // D
    tile_matrix = jnp.array([0, 1, 2, 3] + [4] * repeat + [5] * repeat, dtype=jnp.int32)
    choose = (tile_matrix[:, None] == jnp.arange(7, dtype=jnp.int32)[None, :]).astype(jnp.int32)
    tile_owner = jnp.sum(choose * owners[None, :], axis=1)
    position = jnp.arange(tile_matrix.shape[0], dtype=jnp.int32)
    before = (tile_owner[None, :] == tile_owner[:, None]) & (position[None, :] < position[:, None])
    slot_index = jnp.sum(before.astype(jnp.int32), axis=1)
    return (tile_owner, slot_index)


def adam_update(grad, param, first, second, occupied, decay_rate):
    first_new = occupied * (beta_one * first + (1.0 - beta_one) * grad)
    second_new = occupied * (beta_two * second + (1.0 - beta_two) * grad * grad)
    correct_one = 1.0 - beta_one**ADAM_STEP
    correct_two = 1.0 - beta_two**ADAM_STEP
    direction = first_new / correct_one / (jnp.sqrt(second_new / correct_two) + adam_eps)
    param_new = occupied * (param - learn_rate * (direction + decay_rate * param))
    return (param_new, first_new, second_new)


def collect(row_shard):
    return lax.all_gather(row_shard, "tensor", axis=0, tiled=True)


def spread_rows(term, row_count):
    return lax.psum_scatter(
        term(jnp.int32(0), row_count * lax.axis_size("tensor")).astype(jnp.bfloat16),
        "tensor",
        scatter_dimension=0,
        tiled=True,
    ).astype(jnp.float32)


def row_product(source, weight, form):

    def term(row_start, row_total):
        return jnp.einsum(form, source, weight, preferred_element_type=jnp.float32)

    return term


def scored(query_block, key_rows, present):
    score_scale = HEAD_DIM ** (-0.5)
    scores = (
        jnp.einsum("qhe,khe->hqk", query_block, key_rows, preferred_element_type=jnp.float32)
        * score_scale
    )
    return jnp.where(present[None, None, :], scores, masked_score)


def attention_forward(queries, key_rows, value_rows, present):
    seq_len, heads_here, head_size = queries.shape
    block_rows = min(512, seq_len)

    def block_forward(query_block):
        scores = scored(query_block, key_rows, present)
        maxima = jnp.max(scores, axis=-1, keepdims=True)
        exponent = jnp.exp(scores - maxima)
        totals = jnp.sum(exponent, axis=-1, keepdims=True)
        attention = (exponent / totals).astype(jnp.bfloat16)
        context = jnp.einsum(
            "hqk,khe->qhe", attention, value_rows, preferred_element_type=jnp.float32
        )
        return (context.astype(jnp.bfloat16), (maxima + jnp.log(totals))[:, :, 0])

    return lax.map(
        block_forward, queries.reshape(seq_len // block_rows, block_rows, heads_here, head_size)
    )


def attention_backward(queries, key_rows, value_rows, present, logsum, context_grad):
    seq_len, heads_here, head_size = queries.shape
    block_rows = min(512, seq_len)
    count_blocks = seq_len // block_rows
    score_scale = HEAD_DIM ** (-0.5)

    def block_backward(running, block_items):
        key_grad, value_grad = running
        query_block, logsum_block, upstream = block_items
        attention = jnp.exp(scored(query_block, key_rows, present) - logsum_block[:, :, None])
        product = jnp.einsum(
            "qhe,khe->hqk", upstream, value_rows, preferred_element_type=jnp.float32
        )
        score_grad = (
            attention * (product - jnp.sum(attention * product, axis=-1, keepdims=True))
        ).astype(jnp.bfloat16)
        query_grad = (
            jnp.einsum("hqk,khe->qhe", score_grad, key_rows, preferred_element_type=jnp.float32)
            * score_scale
        ).astype(jnp.bfloat16)
        key_grad = (
            key_grad
            + jnp.einsum(
                "hqk,qhe->khe", score_grad, query_block, preferred_element_type=jnp.float32
            )
            * score_scale
        )
        value_grad = value_grad + jnp.einsum(
            "hqk,qhe->khe",
            attention.astype(jnp.bfloat16),
            upstream,
            preferred_element_type=jnp.float32,
        )
        return ((key_grad, value_grad), query_grad)

    start_grads = (jnp.zeros(key_rows.shape, jnp.float32), jnp.zeros(value_rows.shape, jnp.float32))
    blocked = (
        queries.reshape(count_blocks, block_rows, heads_here, head_size),
        logsum,
        context_grad.reshape(count_blocks, block_rows, heads_here, head_size),
    )
    (key_grad, value_grad), query_grad = lax.scan(block_backward, start_grads, blocked)
    flat_width = heads_here * head_size
    return (
        query_grad.reshape(seq_len, flat_width),
        key_grad.astype(jnp.bfloat16).reshape(seq_len, flat_width),
        value_grad.astype(jnp.bfloat16).reshape(seq_len, flat_width),
    )


def local(
    tokens,
    weights,
    norms,
    cotangent,
    lengths,
    owners,
    master,
    moment_one,
    moment_two,
    norm_master,
    norm_one,
    norm_two,
):
    tensor_size = lax.axis_size("tensor")
    group_size = lax.axis_size("dp")
    tile_width = D // tensor_size
    hidden_width = FF // tensor_size
    heads_here = tile_width // HEAD_DIM
    row_count = tokens.shape[0]
    seq_len = row_count * tensor_size
    w_mixed = weights[:, : 3 * tile_width]
    w_out = weights[:, 3 * tile_width : 4 * tile_width]
    w_up = weights[:, 4 * tile_width : 4 * tile_width + hidden_width]
    w_down = weights[:, 4 * tile_width + hidden_width :]
    length = lengths[0]
    present = jnp.arange(seq_len) < length
    own_present = lax.axis_index("tensor") * row_count + jnp.arange(row_count) < length
    inputs = tokens[:, 0, :]
    gathered = collect(inputs)
    mixed = jnp.dot(gathered, w_mixed, preferred_element_type=jnp.float32).astype(jnp.bfloat16)
    mixed = mixed.reshape(seq_len, 3, heads_here, HEAD_DIM)
    context, logsum = attention_forward(mixed[:, 0], mixed[:, 1], mixed[:, 2], present)
    context = context.reshape(seq_len, tile_width)
    branch = spread_rows(row_product(context, w_out, "se,de->sd"), row_count)
    first_norm, first_normed, first_inverse = layer_norm_parts(
        inputs.astype(jnp.float32) + branch, norms[0], norms[1]
    )
    first_low = first_norm.astype(jnp.bfloat16)
    gathered_first = collect(first_low)
    hidden_pre = jnp.dot(gathered_first, w_up, preferred_element_type=jnp.float32)
    hidden_pre, hidden = (
        hidden_pre,
        jax.nn.gelu(hidden_pre, approximate=False).astype(jnp.bfloat16),
    )
    feed = spread_rows(row_product(hidden, w_down, "sf,df->sd"), row_count)
    second_norm, second_normed, second_inverse = layer_norm_parts(
        first_norm + feed, norms[2], norms[3]
    )
    seed_grad = cotangent[:, 0, :].astype(jnp.float32) * own_present[:, None].astype(jnp.float32)
    second_grad, gain_two, shift_two = layer_norm_back(
        seed_grad, second_normed, second_inverse, norms[2]
    )
    feed_low = second_grad.astype(jnp.bfloat16)
    gathered_feed = collect(feed_low)
    hidden_grad = jnp.dot(gathered_feed, w_down, preferred_element_type=jnp.float32)
    gelu_back = jax.vjp(partial(jax.nn.gelu, approximate=False), hidden_pre)[1]
    pre_grad = gelu_back(hidden_grad)[0].astype(jnp.bfloat16)
    down_grad = jnp.einsum("sd,sf->df", gathered_feed, hidden, preferred_element_type=jnp.float32)
    up_grad = jnp.einsum("sd,sf->df", gathered_first, pre_grad, preferred_element_type=jnp.float32)
    first_grad = second_grad + spread_rows(row_product(pre_grad, w_up, "sf,df->sd"), row_count)
    branch_grad, gain_one, shift_one = layer_norm_back(
        first_grad, first_normed, first_inverse, norms[0]
    )
    branch_low = branch_grad.astype(jnp.bfloat16)
    gathered_branch = collect(branch_low)
    context_grad = jnp.dot(gathered_branch, w_out, preferred_element_type=jnp.float32).astype(
        jnp.bfloat16
    )
    out_grad = jnp.einsum("sd,se->de", gathered_branch, context, preferred_element_type=jnp.float32)
    query_grad, key_grad, value_grad = attention_backward(
        mixed[:, 0], mixed[:, 1], mixed[:, 2], present, logsum, context_grad
    )
    mixed_grad = jnp.concatenate([query_grad, key_grad, value_grad], axis=1)
    mixed_weight_grad = jnp.einsum(
        "sd,se->de", gathered, mixed_grad, preferred_element_type=jnp.float32
    )
    input_total = branch_grad + spread_rows(
        row_product(mixed_grad, w_mixed, "se,de->sd"), row_count
    )
    input_grad = input_total.astype(jnp.bfloat16)[:, None, :]
    mixed_weight_grad, out_grad, up_grad, down_grad = (
        lax.psum_scatter(mixed_weight_grad, "dp", scatter_dimension=0, tiled=True),
        lax.psum_scatter(out_grad, "dp", scatter_dimension=0, tiled=True),
        lax.psum_scatter(up_grad, "dp", scatter_dimension=0, tiled=True),
        lax.psum_scatter(down_grad, "dp", scatter_dimension=0, tiled=True),
    )
    packed_grad = jnp.concatenate([mixed_weight_grad, out_grad, up_grad, down_grad], axis=1)
    norm_grads = lax.psum(jnp.stack([gain_one, shift_one, gain_two, shift_two]), ("dp", "tensor"))
    device = lax.axis_index("dp")
    tile_owner, slot_index = slot_table(owners)
    capacity = FF // D
    slot_ids = jnp.arange(capacity, dtype=jnp.int32)
    owned = ((tile_owner[None, :] == device) & (slot_index[None, :] == slot_ids[:, None])).astype(
        jnp.float32
    )
    occupied = jnp.sum(owned, axis=1)[None, :, None]
    share_rows = D // group_size
    everyone = jnp.arange(group_size, dtype=jnp.int32)
    owned_every = (
        (tile_owner[None, None, :] == everyone[:, None, None])
        & (slot_index[None, None, :] == slot_ids[None, :, None])
    ).astype(jnp.float32)
    share_tiles = packed_grad.reshape(share_rows, -1, tile_width)
    outgoing = jnp.einsum("xiw,psi->pxsw", share_tiles, owned_every, precision=precise)
    incoming = lax.all_to_all(
        outgoing.astype(jnp.bfloat16), "dp", split_axis=0, concat_axis=0, tiled=True
    ).astype(outgoing.dtype)
    slot_grad = incoming.reshape(D, capacity, tile_width)
    new_master, new_one, new_two = adam_update(
        slot_grad,
        master[0].reshape(D, capacity, tile_width),
        moment_one[0].reshape(D, capacity, tile_width),
        moment_two[0].reshape(D, capacity, tile_width),
        occupied,
        weight_decay,
    )
    rounded_low = new_master.astype(jnp.bfloat16).reshape(
        group_size, share_rows, capacity, tile_width
    )
    returned = lax.all_to_all(rounded_low, "dp", split_axis=0, concat_axis=0, tiled=True)
    placed = jnp.einsum(
        "pxsw,psi->xiw", returned.astype(jnp.float32), owned_every, precision=precise
    )
    row_shard = placed.astype(jnp.bfloat16).reshape(share_rows, -1)
    new_weights = lax.all_gather(row_shard, "dp", axis=0, tiled=True)
    norm_owner = (device == owners[6]).astype(jnp.float32)
    new_norm_master, new_norm_one, new_norm_two = adam_update(
        norm_grads, norm_master[0], norm_one[0], norm_two[0], norm_owner, 0.0
    )
    store_shape = (1, D, capacity * tile_width)
    return (
        second_norm.astype(jnp.bfloat16)[:, None, :],
        input_grad,
        slot_grad.reshape(store_shape),
        new_master.reshape(store_shape),
        new_one.reshape(store_shape),
        new_two.reshape(store_shape),
        new_weights,
        norm_grads,
        new_norm_master[None],
        new_norm_one[None],
        new_norm_two[None],
    )


def solution(mesh):
    in_specs = (
        P("tensor", "dp", None),
        P(None, "tensor"),
        P(),
        P("tensor", "dp", None),
        P("dp"),
        P(),
        P("dp", None, "tensor"),
        P("dp", None, "tensor"),
        P("dp", None, "tensor"),
        P("dp", None, None),
        P("dp", None, None),
        P("dp", None, None),
    )
    out_specs = (
        P("tensor", "dp", None),
        P("tensor", "dp", None),
        P("dp", None, "tensor"),
        P("dp", None, "tensor"),
        P("dp", None, "tensor"),
        P("dp", None, "tensor"),
        P(None, "tensor"),
        P(),
        P("dp", None, None),
        P("dp", None, None),
        P("dp", None, None),
    )
    return jax.shard_map(local, mesh=mesh, in_specs=in_specs, out_specs=out_specs, check_vma=False)
```

profile of v0, /device:TPU:0, one launch (start us, length us, event | category | flops | bytes accessed | tf_op | source)
XLA Modules:
  0.0 1279.9 jit_solution(14837155289518703411)
XLA Ops:
  8.0 85.1 %all-gather.15.cloned.1.call-done = bf16[2048,1,1024]{2,0,1:T(8,128)(2,1)} async-done(((bf16[512,1,1024]{2,0,1:T(8,128)(2,1)}), bf16[2048,1,1024]{2,0,1:T(8,128)(2,1)}) %all-gather.15.cloned.1.call-update) | async-done | bytes 4194320 | tf_op jit(solution)/shard_map/all_gather | solution.py:62
  103.6 50.0 %while.28 = (s32[]{:T(128)}, bf16[4,512,4,64]{1,3,2,0:T(8,128)(2,1)}, f32[4,4,512]{2,1,0:T(4,128)S(1)}, bf16[4,512,4,64]{1,3,2,0:T(8,128)(2,1)S(1)}, bf16[2048,4...) while((s32[]{:T(128)}, ...), condition=%wide.region_3.4_spmd.clone, body=%wide.region_0.3_spmd.clone.sunk | while | flops 1124204544 | bytes 53026924 | solution.py:106
  162.8 74.7 %reduce-scatter.9.cloned.1.call-done = bf16[512,1024]{1,0:T(8,128)(2,1)} async-done(((bf16[2048,1024]{1,0:T(8,128)(2,1)}), bf16[512,1024]{1,0:T(8,128)(2,1)}) %reduce-scatter.9.cloned.1.call-update) | async-done | bytes 1048592 | tf_op jit(solution)/shard_map/reduce_scatter | solution.py:66
  242.5 81.4 %all-gather.7.cloned.1.call-done = bf16[2048,1024]{1,0:T(8,128)(2,1)} async-done(((bf16[512,1024]{1,0:T(8,128)(2,1)}), bf16[2048,1024]{1,0:T(8,128)(2,1)}) %all-gather.7.cloned.1.call-update) | async-done | bytes 4194320 | tf_op jit(solution)/shard_map/all_gather | solution.py:62
  323.9 25.6 %multiply_convert_fusion.1 = (bf16[2048,1024]{1,0:T(8,128)(2,1)S(1)}, f32[2048,1024]{1,0:T(8,128)}, f32[2048,1024]{1,0:T(8,128)}) fusion(bf16[2048,1024]{1,0:T(8,128)(2,1)} %all-gather.7.cloned.1.call-done, bf16[1024,3072]{1,0:T(8,128)(2,1)} %param.18), kind=kOutput, calls=%fused_computation.55 | convolution fusion | flops 4431282176 | bytes 27262976 | tf_op jit(solution)/shard_map/dot_general | solution.py:201
  351.4 7.7 convolution_convert_fusion.3
  359.8 74.7 %reduce-scatter.11.cloned.1.call-done = bf16[512,1024]{1,0:T(8,128)(2,1)} async-done(((bf16[2048,1024]{1,0:T(8,128)(2,1)}), bf16[512,1024]{1,0:T(8,128)(2,1)}) %reduce-scatter.11.cloned.1.call-update) | async-done | bytes 1048592 | tf_op jit(solution)/shard_map/reduce_scatter | solution.py:66
  441.5 81.1 %all-gather.9.cloned.1.call-done = bf16[2048,1024]{1,0:T(8,128)(2,1)} async-done(((bf16[512,1024]{1,0:T(8,128)(2,1)}), bf16[2048,1024]{1,0:T(8,128)(2,1)}) %all-gather.9.cloned.1.call-update) | async-done | bytes 4194320 | tf_op jit(solution)/shard_map/all_gather | solution.py:62
  522.7 13.7 %add_convert_fusion = bf16[2048,1024]{1,0:T(8,128)(2,1)S(1)} fusion(f32[2048,1024]{1,0:T(8,128)} %get-tuple-element.307, f32[2048,1024]{1,0:T(8,128)} %get-tuple-element.325, bf16[2048,1024]{1,0:T(8,128)(2,1)} %all-gather.9.cloned.1.call-done, bf16[1024,3072]{1,0:T(8,128)(2,1)} %param.18), kind=kOutput, calls=%fused_computation.54 | convolution fusion | flops 4324327424 | bytes 27262976 | tf_op jit(solution)/shard_map/dot_general | solution.py:216
  538.4 7.7 convolution_convert_fusion.2
  546.1 75.4 %reduce-scatter.13.cloned.1.call-done = bf16[512,1024]{1,0:T(8,128)(2,1)} async-done(((bf16[2048,1024]{1,0:T(8,128)(2,1)}), bf16[512,1024]{1,0:T(8,128)(2,1)}) %reduce-scatter.13.cloned.1.call-update) | async-done | bytes 1048592 | tf_op jit(solution)/shard_map/reduce_scatter | solution.py:66
  627.9 81.3 %all-gather.11.cloned.1.call-done = bf16[2048,1024]{1,0:T(8,128)(2,1)} async-done(((bf16[512,1024]{1,0:T(8,128)(2,1)}), bf16[2048,1024]{1,0:T(8,128)(2,1)}) %all-gather.11.cloned.1.call-update) | async-done | bytes 4194320 | tf_op jit(solution)/shard_map/all_gather | solution.py:62
  723.4 166.8 %while.29 = (s32[]{:T(128)}, f32[2048,4,64]{0,2,1:T(8,128)}, f32[2048,4,64]{0,2,1:T(8,128)}, bf16[4,512,4,64]{1,3,2,0:T(8,128)(2,1)}, bf16[4,512,4,64]{1,3,2,0:T...) while((s32[]{:T(128)}, f32[2048,4,64]{0,2,1:T(8,128)}, ...), condition=%wide.region_17.18_spmd.clone, body=%wide.region_15.17_spmd.clone.sunk | while | flops 2750152704 | bytes 172294320 | solution.py:152
  733.6 9.5 multiply_reduce_fusion.7
  743.1 10.6 multiply_convert_fusion.4
  774.7 9.5 multiply_reduce_fusion.7
  784.2 10.6 multiply_convert_fusion.4
  816.5 9.5 multiply_reduce_fusion.7
  826.0 10.6 multiply_convert_fusion.4
  858.4 9.5 multiply_reduce_fusion.7
  867.9 10.6 multiply_convert_fusion.4
  900.7 10.0 fusion.137
  911.0 10.2 fusion.138
  927.3 7.3 convolution_convert_fusion.1
  935.5 9.8 reduce-scatter.17.cloned.1.call-done
  946.5 53.9 %reduce-scatter.21.cloned.1.call-done = f32[128,1024]{1,0:T(8,128)} async-done(((f32[1024,1024]{1,0:T(8,128)}), f32[128,1024]{1,0:T(8,128)}) %reduce-scatter.21.cloned.1.call-update) | async-done | bytes 524304 | tf_op jit(solution)/shard_map/reduce_scatter | solution.py:245
  1000.5 55.0 %reduce-scatter.23.cloned.1.call-done = f32[128,1024]{1,0:T(8,128)} async-done(((f32[1024,1024]{1,0:T(8,128)}), f32[128,1024]{1,0:T(8,128)}) %reduce-scatter.23.cloned.1.call-update) | async-done | bytes 524304 | tf_op jit(solution)/shard_map/reduce_scatter | solution.py:246
  1055.4 39.7 %reduce-scatter.19.cloned.1.call-done = f32[128,256]{1,0:T(8,128)} async-done(((f32[1024,256]{1,0:T(8,128)}), f32[128,256]{1,0:T(8,128)}) %reduce-scatter.19.cloned.1.call-update) | async-done | bytes 131088 | tf_op jit(solution)/shard_map/reduce_scatter | solution.py:244
  1140.8 12.7 subtract_multiply_fusion
  1164.5 30.6 %all_to_all.10 = bf16[8,128,4,256]{3,1,2,0:T(8,128)(2,1)S(1)} all-to-all(bf16[8,128,4,256]{3,1,2,0:T(8,128)(2,1)S(1)} %copy.93), channel_id=1, replica_groups=mesh['dp'=8,'tensor'=4] {'dp'}, dimensions={0} | all-to-all | bytes 4194304 | tf_op jit(solution)/shard_map/all_to_all | solution.py:281
  1199.3 40.5 %psum.7 = f32[4,1024]{1,0:T(4,128)S(1)} all-reduce(f32[4,1024]{1,0:T(4,128)S(1)} %pad_maximum_fusion.4), channel_id=1, replica_groups=mesh['dp'=8,'tensor'=4] {'dp','tensor'}, use_global_device_ids=true, to_apply=%region_30.31 | all-reduce | flops 4096 | bytes 32768 | tf_op jit(solution)/shard_map/psum | solution.py:249
  1264.6 8.6 copy.100
  (212 shorter events, 296.2 us)
Async XLA Ops:
  7.2 85.9 %all-gather.15.cloned.1.call-start = ((), (), s32[]{:S(2)}) async-start(), calls=%async_computation.22 | async-start | bytes 5242880 | tf_op jit(solution)/shard_map/all_gather | solution.py:62
  7.9 229.6 %reduce-scatter.9.cloned.1.call-start = ((), (), s32[]{:S(2)}) async-start(), calls=%async_computation.10 | async-start | bytes 5242880 | tf_op jit(solution)/shard_map/reduce_scatter | solution.py:66
  153.6 8.5 copy-start.6
  162.1 75.4 %copy-start.2 = (bf16[512,1,1024]{2,0,1:T(8,128)(2,1)S(1)}, bf16[512,1,1024]{2,0,1:T(8,128)(2,1)}, u32[]{:S(2)}) copy-start(bf16[512,1,1024]{2,0,1:T(8,128)(2,1)} %param.17) | copy-start | bytes 3145732
  162.1 161.8 %all-gather.7.cloned.1.call-start = ((), (), s32[]{:S(2)}) async-start(), calls=%async_computation.11 | async-start | bytes 5242880 | tf_op jit(solution)/shard_map/all_gather | solution.py:62
  242.4 192.1 %reduce-scatter.11.cloned.1.call-start = ((), (), s32[]{:S(2)}) async-start(), calls=%async_computation.12 | async-start | bytes 5242880 | tf_op jit(solution)/shard_map/reduce_scatter | solution.py:66
  359.1 163.5 %all-gather.9.cloned.1.call-start = ((), (), s32[]{:S(2)}) async-start(), calls=%async_computation.13 | async-start | bytes 5242880 | tf_op jit(solution)/shard_map/all_gather | solution.py:62
  441.3 180.2 %reduce-scatter.13.cloned.1.call-start = ((), (), s32[]{:S(2)}) async-start(), calls=%async_computation.14 | async-start | bytes 5242880 | tf_op jit(solution)/shard_map/reduce_scatter | solution.py:66
  546.0 163.2 %all-gather.11.cloned.1.call-start = ((), (), s32[]{:S(2)}) async-start(), calls=%async_computation.15 | async-start | bytes 5242880 | tf_op jit(solution)/shard_map/all_gather | solution.py:62
  621.5 3.8 copy-start.7
  621.5 3.8 copy-start.12
  627.8 317.5 %reduce-scatter.17.cloned.1.call-start = ((), (), s32[]{:S(2)}) async-start(), calls=%async_computation.17 | async-start | bytes 3538944 | tf_op jit(solution)/shard_map/reduce_scatter | solution.py:243
  713.8 9.6 copy-start.4
  753.7 6.9 copy-start
  794.8 6.9 copy-start
  836.7 6.9 copy-start
  878.5 6.9 copy-start
  900.7 99.8 %reduce-scatter.21.cloned.1.call-start = ((), (), s32[]{:S(2)}) async-start(), calls=%async_computation.19 | async-start | bytes 4718592 | tf_op jit(solution)/shard_map/reduce_scatter | solution.py:245
  910.8 144.7 %reduce-scatter.23.cloned.1.call-start = ((), (), s32[]{:S(2)}) async-start(), calls=%async_computation.20 | async-start | bytes 4718592 | tf_op jit(solution)/shard_map/reduce_scatter | solution.py:246
  921.3 173.9 %reduce-scatter.19.cloned.1.call-start = ((), (), s32[]{:S(2)}) async-start(), calls=%async_computation.18 | async-start | bytes 1179648 | tf_op jit(solution)/shard_map/reduce_scatter | solution.py:244
  927.0 335.0 %reduce-scatter.15.cloned.1.call-start = ((), (), s32[]{:S(2)}) async-start(), calls=%async_computation.16 | async-start | bytes 5242880 | tf_op jit(solution)/shard_map/reduce_scatter | solution.py:66
  1104.0 31.0 %all-to-all-start = ((bf16[8,128,4,256]{3,1,2,0:T(8,128)(2,1)}), bf16[8,128,4,256]{3,1,2,0:T(8,128)(2,1)}, u32[]{:S(2)}, u32[]{:S(2)}) async-start(bf16[8,128,4,256]{3,1,2,0:T(8,128)(2,1)} %copy.86), calls=%async_computation.8 | async-start | bytes 4194304 | tf_op jit(solution)/shard_map/all_to_all | solution.py:266
  1108.3 156.2 %all-gather.13.cloned.1.call-start = ((), (), s32[]{:S(2)}) async-start(), calls=%async_computation.21 | async-start | bytes 7077888 | tf_op jit(solution)/shard_map/all_gather | solution.py:286
  1164.4 34.8 %copy-start.16 = (f32[1024]{0:T(1024)S(1)}, f32[1024]{0:T(1024)}, u32[]{:S(2)}) copy-start(f32[1024]{0:T(1024)} %get-tuple-element.257) | copy-start | bytes 12292
  1164.4 34.8 %copy-start.17 = (f32[1024]{0:T(1024)S(1)}, f32[1024]{0:T(1024)}, u32[]{:S(2)}) copy-start(f32[1024]{0:T(1024)} %get-tuple-element.262) | copy-start | bytes 12292
  1164.4 34.8 %copy-start.22 = (f32[1024]{0:T(1024)S(1)}, f32[1024]{0:T(1024)}, u32[]{:S(2)}) copy-start(f32[1024]{0:T(1024)} %get-tuple-element.255) | copy-start | bytes 12292
  1164.4 34.8 %copy-start.23 = (f32[1024]{0:T(1024)S(1)}, f32[1024]{0:T(1024)}, u32[]{:S(2)}) copy-start(f32[1024]{0:T(1024)} %get-tuple-element.260) | copy-start | bytes 12292
  1164.4 75.3 %copy-start.18 = (f32[1,4,1024]{2,1,0:T(4,128)S(1)}, f32[1,4,1024]{2,1,0:T(4,128)}, u32[]{:S(2)}) copy-start(f32[1,4,1024]{2,1,0:T(4,128)} %param.28) | copy-start | bytes 49156
  1164.4 75.3 %copy-start.19 = (f32[1,4,1024]{2,1,0:T(4,128)S(1)}, f32[1,4,1024]{2,1,0:T(4,128)}, u32[]{:S(2)}) copy-start(f32[1,4,1024]{2,1,0:T(4,128)} %param.27) | copy-start | bytes 49156
  1164.4 75.3 %copy-start.20 = (f32[1,4,1024]{2,1,0:T(4,128)S(1)}, f32[1,4,1024]{2,1,0:T(4,128)}, u32[]{:S(2)}) copy-start(f32[1,4,1024]{2,1,0:T(4,128)} %param.26) | copy-start | bytes 49156
  1239.8 6.1 copy-start.15
  1256.5 5.5 copy-start.9
  (14 other events, 27.7 us)
Sparse Core Ops, SparseCore 0:
  9.6 83.4 all-gather.14
  162.2 75.2 reduce-scatter.8
  242.6 81.2 all-gather.6
  359.2 75.2 reduce-scatter.10
  441.4 81.2 all-gather.8
  546.2 75.2 reduce-scatter.12
  628.0 81.2 all-gather.10
  900.8 44.5 reduce-scatter.16
  949.3 51.1 reduce-scatter.20
  1004.2 51.1 reduce-scatter.22
  1059.2 35.9 reduce-scatter.18
  1097.9 76.7 reduce-scatter.14
  1198.1 46.6 all-gather.12
where the time goes:
time: 1290 us; the launch traced here: 1280 us
  waiting for transfers between devices  713 us (55%)
  matrix products  263 us (20%)
  other arithmetic  105 us (8%)
  local copies, waits for them, and re-layouts  104 us (8%)
  blocking collectives  71.1 us (6%)
  between operations  15.8 us (1%)
    all_gather x4, waiting for transfers between devices, collect(): return lax.all_gather(row_shard, 'tensor', axis=0, tiled=True)  329 us
    reduce_scatter x4, waiting for transfers between devices, spread_rows(): lax.psum_scatter(term(jnp.int32(0), row_count * lax.axis_size('tensor'))....  225 us
    unnamed x72, local copies, waits for them, and re-layouts  63.2 us
    reduce_scatter x1, waiting for transfers between devices, local(): lax.psum_scatter(down_grad, 'dp', scatter_dimension=0, tiled=True)  55 us
    reduce_scatter x1, waiting for transfers between devices, local(): lax.psum_scatter(up_grad, 'dp', scatter_dimension=0, tiled=True)  53.9 us
    convert_element_type x4, other arithmetic, block_backward(): score_grad = (attention * (product - jnp.sum(attention * product, axis=-1...  42.5 us
    psum x1, blocking collectives, local(): lax.psum(jnp.stack([gain_one, shift_one, gain_two, shift_two]), ('dp', 't...  40.5 us
    reduce_scatter x1, waiting for transfers between devices, local(): lax.psum_scatter(out_grad, 'dp', scatter_dimension=0, tiled=True)  39.7 us
  transfers between devices with their start and end apart: 14, of which 12 were waited for; matrix products, arithmetic and copies ran while one was open for 10% of the time, Pallas kernels for 0%

commit v1 on v0

--- a/solution.py
+++ b/solution.py
@@ -18,6 +18,22 @@
 masked_score = -1e30
 
 
+def collect_2(x, axis, dim):
+    ways, here, step = (lax.axis_size(axis), lax.axis_index(axis), x.shape[dim])
+    dims = [n * ways if d == dim else n for d, n in enumerate(x.shape)]
+    full = lax.dynamic_update_slice_in_dim(jnp.zeros(dims, x.dtype), x, here * step, axis=dim)
+    going_up = going_down = x
+    for far in range(1, ways // 2 + 1):
+        going_up = lax.ppermute(going_up, axis, [(d, (d + 1) % ways) for d in range(ways)])
+        full = lax.dynamic_update_slice_in_dim(full, going_up, (here - far) % ways * step, axis=dim)
+        if 2 * far < ways:
+            going_down = lax.ppermute(going_down, axis, [(d, (d - 1) % ways) for d in range(ways)])
+            full = lax.dynamic_update_slice_in_dim(
+                full, going_down, (here + far) % ways * step, axis=dim
+            )
+    return full
+
+
 def layer_norm_parts(value, gain, shift):
     average = jnp.mean(value, axis=-1, keepdims=True)
     centred = value - average
@@ -59,7 +75,7 @@
 
 
 def collect(row_shard):
-    return lax.all_gather(row_shard, "tensor", axis=0, tiled=True)
+    return collect_2(row_shard, "tensor", 0)
 
 
 def spread_rows(term, row_count):

time: 1290 us -> 1110 us (0.86)
  waiting for transfers between devices: 713 us -> 452 us
  starting transfers between devices: 6.2 us -> 82.5 us
    all_gather x4 -> x0, waiting for transfers between devices: 329 us -> none  [collect(): return lax.all_gather(row_shard, 'tensor', axis=0, tiled=True)]
    ppermute x0 -> x12, waiting for transfers between devices: none -> 206 us  [the longest x8 181 us: collect_2(): lax.ppermute(going_up, axis, [(d, (d + 1) % ways) for d in range(ways)])]
    ppermute x0 -> x12, starting transfers between devices: none -> 77 us  [the longest x8 67.9 us: collect_2(): lax.ppermute(going_up, axis, [(d, (d + 1) % ways) for d in range(ways)])]
    reduce_scatter x1, waiting for transfers between devices: 55 us -> 0.02 us  [local(): lax.psum_scatter(down_grad, 'dp', scatter_dimension=0, tiled=True)]
    reduce_scatter x1, waiting for transfers between devices: 53.9 us -> 0.02 us  [local(): lax.psum_scatter(up_grad, 'dp', scatter_dimension=0, tiled=True)]
    reduce_scatter x1, waiting for transfers between devices: 39.7 us -> 0.02 us  [local(): lax.psum_scatter(out_grad, 'dp', scatter_dimension=0, tiled=True)]
    reduce_scatter x1, waiting for transfers between devices: 9.84 us -> 38.4 us  [local(): lax.psum_scatter(mixed_weight_grad, 'dp', scatter_dimension=0, tiled=True)]
    reduce_scatter x4, waiting for transfers between devices: 225 us -> 207 us  [spread_rows(): lax.psum_scatter(term(jnp.int32(0), row_count * lax.axis_size('tensor'))....]
  transfers between devices with their start and end apart: 14 -> 22, of which waited for: 12 -> 17; matrix products, arithmetic and copies ran while one was open for 10% -> 29% of each run, Pallas kernels for 0% -> 0%
where the time goes in v1:
time: 1110 us; the launch traced here: 1100 us
  waiting for transfers between devices  452 us (41%)
  matrix products  259 us (23%)
  local copies, waits for them, and re-layouts  111 us (10%)
  other arithmetic  107 us (10%)
  starting transfers between devices  82.5 us (7%)
  blocking collectives  71 us (6%)
  between operations  16.1 us (1%)
    reduce_scatter x4, waiting for transfers between devices, spread_rows(): lax.psum_scatter(term(jnp.int32(0), row_count * lax.axis_size('tensor'))....  207 us
    ppermute x8, waiting for transfers between devices, collect_2(): lax.ppermute(going_up, axis, [(d, (d + 1) % ways) for d in range(ways)])  181 us
    ppermute x8, starting transfers between devices, collect_2(): lax.ppermute(going_up, axis, [(d, (d + 1) % ways) for d in range(ways)])  67.9 us
    unnamed x90, local copies, waits for them, and re-layouts  62.4 us
    convert_element_type x4, other arithmetic, block_backward(): score_grad = (attention * (product - jnp.sum(attention * product, axis=-1...  42.8 us
    psum x1, blocking collectives, local(): lax.psum(jnp.stack([gain_one, shift_one, gain_two, shift_two]), ('dp', 't...  40.4 us
    reduce_scatter x1, waiting for transfers between devices, local(): lax.psum_scatter(mixed_weight_grad, 'dp', scatter_dimension=0, tiled=True)  38.4 us
    dot_general x4, matrix products, block_backward(): jnp.einsum('qhe,khe->hqk', upstream, value_rows, preferred_element_type=j...  38 us
  transfers between devices with their start and end apart: 22, of which 17 were waited for; matrix products, arithmetic and copies ran while one was open for 29% of the time, Pallas kernels for 0%

profile of v1, /device:TPU:0, one launch (start us, length us, event | category | flops | bytes accessed | tf_op | source)
XLA Modules:
  0.0 1098.5 jit_solution(18283304996161773574)
XLA Ops:
  12.4 24.2 %collective-permute-done = bf16[512,1024]{1,0:T(8,128)(2,1)S(1)} collective-permute-done((bf16[512,1024]{1,0:T(8,128)(2,1)}, bf16[512,1024]{1,0:T(8,128)(2,1)S(1)}, u32[]{:S(2)}, u32[]{:S(2)}) %collective-permute-start) | collective-permute-done | bytes 1048608 | tf_op jit(solution)/shard_map/ppermute | solution.py:27
  37.4 20.5 %collective-permute-done.1 = bf16[512,1024]{1,0:T(8,128)(2,1)S(1)} collective-permute-done((bf16[512,1024]{1,0:T(8,128)(2,1)}, bf16[512,1024]{1,0:T(8,128)(2,1)S(1)}, u32[]{:S(2)}, u32[]{:S(2)}) %collective-permute-start.1) | collective-permute-done | bytes 1048608 | tf_op jit(solution)/shard_map/ppermute | solution.py:30
  58.0 22.8 %collective-permute-done.2 = bf16[512,1024]{1,0:T(8,128)(2,1)} collective-permute-done((bf16[512,1024]{1,0:T(8,128)(2,1)S(1)}, bf16[512,1024]{1,0:T(8,128)(2,1)}, u32[]{:S(2)}, u32[]{:S(2)}) %collective-permute-start.2) | collective-permute-done | bytes 1048608 | tf_op jit(solution)/shard_map/ppermute | solution.py:27
  92.9 52.3 %while.28 = (s32[]{:T(128)}, bf16[4,512,4,64]{1,3,2,0:T(8,128)(2,1)}, f32[4,4,512]{2,1,0:T(4,128)}, bf16[4,512,4,64]{1,3,2,0:T(8,128)(2,1)S(1)}, bf16[2048,4,64]...) while((s32[]{:T(128)}, bf16[4,512,4,64]{1,3,2,0:T(8,128)(2,1)}, ...), condition=%wide.region_3.4_spmd.clone, body=%wide.region_0.3_spmd.clone.sunk | while | flops 1124204544 | bytes 53026924 | solution.py:122
  154.4 75.6 %reduce-scatter.9.cloned.1.call-done = bf16[512,1024]{1,0:T(8,128)(2,1)} async-done(((bf16[2048,1024]{1,0:T(8,128)(2,1)}), bf16[512,1024]{1,0:T(8,128)(2,1)}) %reduce-scatter.9.cloned.1.call-update) | async-done | bytes 1048592 | tf_op jit(solution)/shard_map/reduce_scatter | solution.py:82
  238.4 24.1 %collective-permute-done.3 = bf16[512,1024]{1,0:T(8,128)(2,1)S(1)} collective-permute-done((bf16[512,1024]{1,0:T(8,128)(2,1)S(1)}, bf16[512,1024]{1,0:T(8,128)(2,1)S(1)}, u32[]{:S(2)}, u32[]{:S(2)}) %collective-permute-start.3) | collective-permute-done | bytes 1048608 | tf_op jit(solution)/shard_map/ppermute | solution.py:27
  262.5 20.0 %collective-permute-start.5 = (bf16[512,1024]{1,0:T(8,128)(2,1)S(1)}, bf16[512,1024]{1,0:T(8,128)(2,1)S(1)}, u32[]{:S(2)}, u32[]{:S(2)}) collective-permute-start(bf16[512,1024]{1,0:T(8,128)(2,1)S(1)} %collective-permute-done.3), channel_id=1, source_target_pairs={{0,1},{1,2},{2,3},{3,0},{4,5},{5,6},{6,7},{7,4},{8,9},{9,10},{10,1... | collective-permute-start | bytes 3145736 | tf_op jit(solution)/shard_map/ppermute | solution.py:27
  284.7 21.3 %collective-permute-done.5 = bf16[512,1024]{1,0:T(8,128)(2,1)S(1)} collective-permute-done((bf16[512,1024]{1,0:T(8,128)(2,1)S(1)}, bf16[512,1024]{1,0:T(8,128)(2,1)S(1)}, u32[]{:S(2)}, u32[]{:S(2)}) %collective-permute-start.5) | collective-permute-done | bytes 1048608 | tf_op jit(solution)/shard_map/ppermute | solution.py:27
  306.1 26.6 %multiply_convert_fusion.1 = (bf16[2048,1024]{1,0:T(8,128)(2,1)S(1)}, f32[2048,1024]{1,0:T(8,128)}, f32[2048,1024]{1,0:T(8,128)}) fusion(bf16[2048,1024]{1,0:T(8,128)(2,1)S(1)} %constant_dynamic-update-slice_fusion.8, bf16[1024,3072]{1,0:T(8,128)(2,1)S(1)} %bitcast.259), kind=kOutput, calls=%fused_computation.55 | convolution fusion | flops 4431282176 | bytes 27262976 | tf_op jit(solution)/shard_map/dot_general | solution.py:217
  341.8 75.5 %reduce-scatter.11.cloned.1.call-done = bf16[512,1024]{1,0:T(8,128)(2,1)} async-done(((bf16[2048,1024]{1,0:T(8,128)(2,1)}), bf16[512,1024]{1,0:T(8,128)(2,1)}) %reduce-scatter.11.cloned.1.call-update) | async-done | bytes 1048592 | tf_op jit(solution)/shard_map/reduce_scatter | solution.py:82
  428.8 24.1 %collective-permute-done.6 = bf16[512,1024]{1,0:T(8,128)(2,1)S(1)} collective-permute-done((bf16[512,1024]{1,0:T(8,128)(2,1)S(1)}, bf16[512,1024]{1,0:T(8,128)(2,1)S(1)}, u32[]{:S(2)}, u32[]{:S(2)}) %collective-permute-start.6) | collective-permute-done | bytes 1048608 | tf_op jit(solution)/shard_map/ppermute | solution.py:27
  452.9 20.2 %collective-permute-start.8 = (bf16[512,1024]{1,0:T(8,128)(2,1)S(1)}, bf16[512,1024]{1,0:T(8,128)(2,1)S(1)}, u32[]{:S(2)}, u32[]{:S(2)}) collective-permute-start(bf16[512,1024]{1,0:T(8,128)(2,1)S(1)} %collective-permute-done.6), channel_id=1, source_target_pairs={{0,1},{1,2},{2,3},{3,0},{4,5},{5,6},{6,7},{7,4},{8,9},{9,10},{10,1... | collective-permute-start | bytes 3145736 | tf_op jit(solution)/shard_map/ppermute | solution.py:27
  475.2 21.2 %collective-permute-done.8 = bf16[512,1024]{1,0:T(8,128)(2,1)S(1)} collective-permute-done((bf16[512,1024]{1,0:T(8,128)(2,1)S(1)}, bf16[512,1024]{1,0:T(8,128)(2,1)S(1)}, u32[]{:S(2)}, u32[]{:S(2)}) %collective-permute-start.8) | collective-permute-done | bytes 1048608 | tf_op jit(solution)/shard_map/ppermute | solution.py:27
  496.5 12.5 %add_convert_fusion = bf16[2048,1024]{1,0:T(8,128)(2,1)S(1)} fusion(f32[2048,1024]{1,0:T(8,128)} %get-tuple-element.309, f32[2048,1024]{1,0:T(8,128)} %get-tuple-element.329, bf16[2048,1024]{1,0:T(8,128)(2,1)S(1)} %constant_dynamic-update-slice_fusion.4, bf16[1024,3072]{1,0:T(8,128)(2,1)S(1)} %bitcast.261), kind=kOutput, calls=%fused_computation.54 | convolution fusion | flops 4324327424 | bytes 27262976 | tf_op jit(solution)/shard_map/dot_general | solution.py:232
  517.4 10.0 fusion.127
  527.9 10.0 fusion.128
  538.0 55.7 %reduce-scatter.13.cloned.1.call-done = bf16[512,1024]{1,0:T(8,128)(2,1)} async-done(((bf16[2048,1024]{1,0:T(8,128)(2,1)}), bf16[512,1024]{1,0:T(8,128)(2,1)}) %reduce-scatter.13.cloned.1.call-update) | async-done | bytes 1048592 | tf_op jit(solution)/shard_map/reduce_scatter | solution.py:82
  606.1 24.1 %collective-permute-done.9 = bf16[512,1024]{1,0:T(8,128)(2,1)S(1)} collective-permute-done((bf16[512,1024]{1,0:T(8,128)(2,1)S(1)}, bf16[512,1024]{1,0:T(8,128)(2,1)S(1)}, u32[]{:S(2)}, u32[]{:S(2)}) %collective-permute-start.9) | collective-permute-done | bytes 1048608 | tf_op jit(solution)/shard_map/ppermute | solution.py:27
  630.2 20.0 %collective-permute-start.11 = (bf16[512,1024]{1,0:T(8,128)(2,1)S(1)}, bf16[512,1024]{1,0:T(8,128)(2,1)S(1)}, u32[]{:S(2)}, u32[]{:S(2)}) collective-permute-start(bf16[512,1024]{1,0:T(8,128)(2,1)S(1)} %collective-permute-done.9), channel_id=1, source_target_pairs={{0,1},{1,2},{2,3},{3,0},{4,5},{5,6},{6,7},{7,4},{8,9},{9,10},{10,1... | collective-permute-start | bytes 3145736 | tf_op jit(solution)/shard_map/ppermute | solution.py:27
  654.6 19.1 %collective-permute-done.11 = bf16[512,1024]{1,0:T(8,128)(2,1)S(1)} collective-permute-done((bf16[512,1024]{1,0:T(8,128)(2,1)S(1)}, bf16[512,1024]{1,0:T(8,128)(2,1)S(1)}, u32[]{:S(2)}, u32[]{:S(2)}) %collective-permute-start.11) | collective-permute-done | bytes 1048608 | tf_op jit(solution)/shard_map/ppermute | solution.py:27
  687.9 169.5 %while.29 = (s32[]{:T(128)}, f32[2048,4,64]{0,2,1:T(8,128)}, f32[2048,4,64]{0,2,1:T(8,128)}, bf16[4,512,4,64]{1,3,2,0:T(8,128)(2,1)}, bf16[4,512,4,64]{1,3,2,0:T...) while((s32[]{:T(128)}, f32[2048,4,64]{0,2,1:T(8,128)}, ...), condition=%wide.region_17.18_spmd.clone, body=%wide.region_15.17_spmd.clone.sunk | while | flops 2750152704 | bytes 172294320 | solution.py:168
  707.9 10.9 multiply_convert_fusion.4
  740.4 9.5 multiply_reduce_fusion.7
  749.9 10.7 multiply_convert_fusion.4
  783.0 9.5 multiply_reduce_fusion.7
  792.5 10.7 multiply_convert_fusion.4
  825.6 9.5 multiply_reduce_fusion.7
  835.1 10.7 multiply_convert_fusion.4
  875.3 38.4 %reduce-scatter.17.cloned.1.call-done = f32[128,768]{1,0:T(8,128)} async-done(((f32[1024,768]{1,0:T(8,128)}), f32[128,768]{1,0:T(8,128)}) %reduce-scatter.17.cloned.1.call-update) | async-done | bytes 393232 | tf_op jit(solution)/shard_map/reduce_scatter | solution.py:259
  959.4 12.7 %subtract_multiply_fusion = (f32[1,1024,1024]{1,2,0:T(8,128)}, f32[1,1024,1024]{1,2,0:T(8,128)}, f32[1,1024,1024]{1,2,0:T(8,128)}, f32[128,8,8,128]{3,1,2,0:T(8,128)S(1)}, f32[128,8,8,128]{3,1,2,0:T(8,128)S(1)}) fusion(f32[1,1024,1024]{1,2,0:T(8,128)} %copy.87, f32[1024]{0:T(1024)S(1)} %bitcast.266, f32[1,1024,1024]{1,2,0:T(8,128)} %reshape_reshape.3, ...), kind=kLoop, calls=%fused_computation.81 | loop fusion | flops 18874368 | bytes 37752832 | tf_op jit(solution)/shard_map/mul | solution.py:73
  983.1 30.6 %all_to_all.10 = bf16[8,128,4,256]{3,1,2,0:T(8,128)(2,1)S(1)} all-to-all(bf16[8,128,4,256]{3,1,2,0:T(8,128)(2,1)S(1)} %copy.89), channel_id=1, replica_groups=mesh['dp'=8,'tensor'=4] {'dp'}, dimensions={0} | all-to-all | bytes 4194304 | tf_op jit(solution)/shard_map/all_to_all | solution.py:297
  1017.9 40.4 %psum.7 = f32[4,1024]{1,0:T(4,128)S(1)} all-reduce(f32[4,1024]{1,0:T(4,128)S(1)} %pad_maximum_fusion.4), channel_id=1, replica_groups=mesh['dp'=8,'tensor'=4] {'dp','tensor'}, use_global_device_ids=true, to_apply=%region_30.31 | all-reduce | flops 4096 | bytes 32768 | tf_op jit(solution)/shard_map/psum | solution.py:265
  (260 shorter events, 361.2 us)
Async XLA Ops:
  7.2 222.8 %reduce-scatter.9.cloned.1.call-start = ((), (), s32[]{:S(2)}) async-start(), calls=%async_computation.10 | async-start | bytes 5242880 | tf_op jit(solution)/shard_map/reduce_scatter | solution.py:82
  7.2 29.4 %collective-permute-start = (bf16[512,1024]{1,0:T(8,128)(2,1)}, bf16[512,1024]{1,0:T(8,128)(2,1)S(1)}, u32[]{:S(2)}, u32[]{:S(2)}) collective-permute-start(bf16[512,1024]{1,0:T(8,128)(2,1)} %bitcast.237), channel_id=1, source_target_pairs={{0,1},{1,2},{2,3},{3,0},{4,5},{5,6},{6,7},{7,4},{8,9},{9,10},{10,1... | collective-permute-start | bytes 3145736 | tf_op jit(solution)/shard_map/ppermute | solution.py:27
  10.3 47.5 %collective-permute-start.1 = (bf16[512,1024]{1,0:T(8,128)(2,1)}, bf16[512,1024]{1,0:T(8,128)(2,1)S(1)}, u32[]{:S(2)}, u32[]{:S(2)}) collective-permute-start(bf16[512,1024]{1,0:T(8,128)(2,1)} %bitcast.238), channel_id=1, source_target_pairs={{0,3},{1,0},{2,1},{3,2},{4,7},{5,4},{6,5},{7,6},{8,11},{9,8},{10,9... | collective-permute-start | bytes 3145736 | tf_op jit(solution)/shard_map/ppermute | solution.py:30
  36.6 44.2 %collective-permute-start.2 = (bf16[512,1024]{1,0:T(8,128)(2,1)S(1)}, bf16[512,1024]{1,0:T(8,128)(2,1)}, u32[]{:S(2)}, u32[]{:S(2)}) collective-permute-start(bf16[512,1024]{1,0:T(8,128)(2,1)S(1)} %collective-permute-done), channel_id=1, source_target_pairs={{0,1},{1,2},{2,3},{3,0},{4,5},{5,6},{6,7},{7,4},{8,9},{9,10},{10,1... | collective-permute-start | bytes 3145736 | tf_op jit(solution)/shard_map/ppermute | solution.py:27
  153.7 76.3 %copy-start.5 = (bf16[512,1,1024]{2,0,1:T(8,128)(2,1)S(1)}, bf16[512,1,1024]{2,0,1:T(8,128)(2,1)}, u32[]{:S(2)}) copy-start(bf16[512,1,1024]{2,0,1:T(8,128)(2,1)} %param.17) | copy-start | bytes 3145732
  153.7 263.6 %reduce-scatter.11.cloned.1.call-start = ((), (), s32[]{:S(2)}) async-start(), calls=%async_computation.11 | async-start | bytes 5242880 | tf_op jit(solution)/shard_map/reduce_scatter | solution.py:82
  233.4 72.7 %slice-start = ((s8[6291456]{0:T(1024)(128)(4,1)}), s8[4194304]{0:T(1024)(128)(4,1)S(1)}, s32[]{:S(2)}) async-start(s8[6291456]{0:T(1024)(128)(4,1)} %bitcast.258), calls=%async_computation.19 | async-start | bytes 8388608
  233.9 72.2 %slice-start.1 = ((s8[6291456]{0:T(1024)(128)(4,1)}), s8[2097152]{0:T(1024)(128)(4,1)S(1)}, s32[]{:S(2)}) async-start(s8[6291456]{0:T(1024)(128)(4,1)} %bitcast.258), calls=%async_computation.20 | async-start | bytes 4194304
  234.5 28.0 %collective-permute-start.3 = (bf16[512,1024]{1,0:T(8,128)(2,1)S(1)}, bf16[512,1024]{1,0:T(8,128)(2,1)S(1)}, u32[]{:S(2)}, u32[]{:S(2)}) collective-permute-start(bf16[512,1024]{1,0:T(8,128)(2,1)S(1)} %get-tuple-element.311), channel_id=1, source_target_pairs={{0,1},{1,2},{2,3},{3,0},{4,5},{5,6},{6,7},{7,4},{8,9},{9,10},{10,1... | collective-permute-start | bytes 3145736 | tf_op jit(solution)/shard_map/ppermute | solution.py:27
  236.0 48.6 %collective-permute-start.4 = (bf16[512,1024]{1,0:T(8,128)(2,1)S(1)}, bf16[512,1024]{1,0:T(8,128)(2,1)S(1)}, u32[]{:S(2)}, u32[]{:S(2)}) collective-permute-start(bf16[512,1024]{1,0:T(8,128)(2,1)S(1)} %get-tuple-element.311), channel_id=1, source_target_pairs={{0,3},{1,0},{2,1},{3,2},{4,7},{5,4},{6,5},{7,6},{8,11},{9,8},{10,9... | collective-permute-start | bytes 3145736 | tf_op jit(solution)/shard_map/ppermute | solution.py:30
  262.5 43.5 %collective-permute-start.5 = (bf16[512,1024]{1,0:T(8,128)(2,1)S(1)}, bf16[512,1024]{1,0:T(8,128)(2,1)S(1)}, u32[]{:S(2)}, u32[]{:S(2)}) collective-permute-start(bf16[512,1024]{1,0:T(8,128)(2,1)S(1)} %collective-permute-done.3), channel_id=1, source_target_pairs={{0,1},{1,2},{2,3},{3,0},{4,5},{5,6},{6,7},{7,4},{8,9},{9,10},{10,1... | collective-permute-start | bytes 3145736 | tf_op jit(solution)/shard_map/ppermute | solution.py:27
  341.0 78.7 %copy-start.19 = (bf16[512,1,1024]{2,0,1:T(8,128)(2,1)S(1)}, bf16[512,1,1024]{2,0,1:T(8,128)(2,1)}, u32[]{:S(2)}) copy-start(bf16[512,1,1024]{2,0,1:T(8,128)(2,1)} %param.20) | copy-start | bytes 3145732
  341.0 252.7 %reduce-scatter.13.cloned.1.call-start = ((), (), s32[]{:S(2)}) async-start(), calls=%async_computation.12 | async-start | bytes 5242880 | tf_op jit(solution)/shard_map/reduce_scatter | solution.py:82
  422.3 74.2 %slice-start.2 = ((s8[6291456]{0:T(1024)(128)(4,1)}), s8[4194304]{0:T(1024)(128)(4,1)S(1)}, s32[]{:S(2)}) async-start(s8[6291456]{0:T(1024)(128)(4,1)} %bitcast.260), calls=%async_computation.21 | async-start | bytes 8388608
  422.8 73.7 %slice-start.3 = ((s8[6291456]{0:T(1024)(128)(4,1)}), s8[2097152]{0:T(1024)(128)(4,1)S(1)}, s32[]{:S(2)}) async-start(s8[6291456]{0:T(1024)(128)(4,1)} %bitcast.260), calls=%async_computation.22 | async-start | bytes 4194304
  425.0 27.9 %collective-permute-start.6 = (bf16[512,1024]{1,0:T(8,128)(2,1)S(1)}, bf16[512,1024]{1,0:T(8,128)(2,1)S(1)}, u32[]{:S(2)}, u32[]{:S(2)}) collective-permute-start(bf16[512,1024]{1,0:T(8,128)(2,1)S(1)} %get-tuple-element.304), channel_id=1, source_target_pairs={{0,1},{1,2},{2,3},{3,0},{4,5},{5,6},{6,7},{7,4},{8,9},{9,10},{10,1... | collective-permute-start | bytes 3145736 | tf_op jit(solution)/shard_map/ppermute | solution.py:27
  426.4 48.6 %collective-permute-start.7 = (bf16[512,1024]{1,0:T(8,128)(2,1)S(1)}, bf16[512,1024]{1,0:T(8,128)(2,1)S(1)}, u32[]{:S(2)}, u32[]{:S(2)}) collective-permute-start(bf16[512,1024]{1,0:T(8,128)(2,1)S(1)} %get-tuple-element.304), channel_id=1, source_target_pairs={{0,3},{1,0},{2,1},{3,2},{4,7},{5,4},{6,5},{7,6},{8,11},{9,8},{10,9... | collective-permute-start | bytes 3145736 | tf_op jit(solution)/shard_map/ppermute | solution.py:30
  452.9 43.5 %collective-permute-start.8 = (bf16[512,1024]{1,0:T(8,128)(2,1)S(1)}, bf16[512,1024]{1,0:T(8,128)(2,1)S(1)}, u32[]{:S(2)}, u32[]{:S(2)}) collective-permute-start(bf16[512,1024]{1,0:T(8,128)(2,1)S(1)} %collective-permute-done.6), channel_id=1, source_target_pairs={{0,1},{1,2},{2,3},{3,0},{4,5},{5,6},{6,7},{7,4},{8,9},{9,10},{10,1... | collective-permute-start | bytes 3145736 | tf_op jit(solution)/shard_map/ppermute | solution.py:27
  517.4 357.8 %reduce-scatter.21.cloned.1.call-start = ((), (), s32[]{:S(2)}) async-start(), calls=%async_computation.16 | async-start | bytes 4718592 | tf_op jit(solution)/shard_map/reduce_scatter | solution.py:261
  527.4 347.8 %reduce-scatter.23.cloned.1.call-start = ((), (), s32[]{:S(2)}) async-start(), calls=%async_computation.17 | async-start | bytes 4718592 | tf_op jit(solution)/shard_map/reduce_scatter | solution.py:262
  538.0 337.3 %reduce-scatter.19.cloned.1.call-start = ((), (), s32[]{:S(2)}) async-start(), calls=%async_computation.15 | async-start | bytes 1179648 | tf_op jit(solution)/shard_map/reduce_scatter | solution.py:260
  602.3 27.9 %collective-permute-start.9 = (bf16[512,1024]{1,0:T(8,128)(2,1)S(1)}, bf16[512,1024]{1,0:T(8,128)(2,1)S(1)}, u32[]{:S(2)}, u32[]{:S(2)}) collective-permute-start(bf16[512,1024]{1,0:T(8,128)(2,1)S(1)} %get-tuple-element.301), channel_id=1, source_target_pairs={{0,1},{1,2},{2,3},{3,0},{4,5},{5,6},{6,7},{7,4},{8,9},{9,10},{10,1... | collective-permute-start | bytes 3145736 | tf_op jit(solution)/shard_map/ppermute | solution.py:27
  603.8 48.6 %collective-permute-start.10 = (bf16[512,1024]{1,0:T(8,128)(2,1)S(1)}, bf16[512,1024]{1,0:T(8,128)(2,1)}, u32[]{:S(2)}, u32[]{:S(2)}) collective-permute-start(bf16[512,1024]{1,0:T(8,128)(2,1)S(1)} %get-tuple-element.301), channel_id=1, source_target_pairs={{0,3},{1,0},{2,1},{3,2},{4,7},{5,4},{6,5},{7,6},{8,11},{9,8},{10,9... | collective-permute-start | bytes 3145736 | tf_op jit(solution)/shard_map/ppermute | solution.py:30
  630.2 43.5 %collective-permute-start.11 = (bf16[512,1024]{1,0:T(8,128)(2,1)S(1)}, bf16[512,1024]{1,0:T(8,128)(2,1)S(1)}, u32[]{:S(2)}, u32[]{:S(2)}) collective-permute-start(bf16[512,1024]{1,0:T(8,128)(2,1)S(1)} %collective-permute-done.9), channel_id=1, source_target_pairs={{0,1},{1,2},{2,3},{3,0},{4,5},{5,6},{6,7},{7,4},{8,9},{9,10},{10,1... | collective-permute-start | bytes 3145736 | tf_op jit(solution)/shard_map/ppermute | solution.py:27
  686.6 227.0 %reduce-scatter.17.cloned.1.call-start = ((), (), s32[]{:S(2)}) async-start(), calls=%async_computation.14 | async-start | bytes 3538944 | tf_op jit(solution)/shard_map/reduce_scatter | solution.py:259
  867.7 212.9 %reduce-scatter.15.cloned.1.call-start = ((), (), s32[]{:S(2)}) async-start(), calls=%async_computation.13 | async-start | bytes 5242880 | tf_op jit(solution)/shard_map/reduce_scatter | solution.py:82
  922.6 31.0 %all-to-all-start = ((bf16[8,128,4,256]{3,1,2,0:T(8,128)(2,1)}), bf16[8,128,4,256]{3,1,2,0:T(8,128)(2,1)}, u32[]{:S(2)}, u32[]{:S(2)}) async-start(bf16[8,128,4,256]{3,1,2,0:T(8,128)(2,1)} %copy.82), calls=%async_computation.8 | async-start | bytes 4194304 | tf_op jit(solution)/shard_map/all_to_all | solution.py:282
  927.0 156.2 %all-gather.2.cloned.1.call-start = ((), (), s32[]{:S(2)}) async-start(), calls=%async_computation.18 | async-start | bytes 7077888 | tf_op jit(solution)/shard_map/all_gather | solution.py:302
  983.0 34.8 %copy-start.26 = (f32[1024]{0:T(1024)S(1)}, f32[1024]{0:T(1024)}, u32[]{:S(2)}) copy-start(f32[1024]{0:T(1024)} %get-tuple-element.257) | copy-start | bytes 12292
  983.0 75.3 %copy-start.22 = (f32[1,4,1024]{2,1,0:T(4,128)S(1)}, f32[1,4,1024]{2,1,0:T(4,128)}, u32[]{:S(2)}) copy-start(f32[1,4,1024]{2,1,0:T(4,128)} %param.28) | copy-start | bytes 49156
  983.0 75.3 %copy-start.23 = (f32[1,4,1024]{2,1,0:T(4,128)S(1)}, f32[1,4,1024]{2,1,0:T(4,128)}, u32[]{:S(2)}) copy-start(f32[1,4,1024]{2,1,0:T(4,128)} %param.27) | copy-start | bytes 49156
  983.1 75.3 %copy-start.24 = (f32[1,4,1024]{2,1,0:T(4,128)S(1)}, f32[1,4,1024]{2,1,0:T(4,128)}, u32[]{:S(2)}) copy-start(f32[1,4,1024]{2,1,0:T(4,128)} %param.26) | copy-start | bytes 49156
  (31 other events, 281.1 us)
Sparse Core Ops, SparseCore 0:
  153.8 76.1 reduce-scatter.8
  341.1 76.1 reduce-scatter.10
  517.5 76.1 reduce-scatter.12
  596.9 51.6 reduce-scatter.20
  652.4 51.1 reduce-scatter.22
  706.6 35.9 reduce-scatter.18
  867.8 45.7 reduce-scatter.16
  916.5 76.7 reduce-scatter.14
  1016.7 46.6 all-gather.1
